TPU v7x, 512 devices: a whole 4x8x8 slice. The times are simulated.
512 devices in a mesh: prow: 8 (over z), pcol: 64 (over y, x, core).
Axes of the slice: x: 4, y: 8, z: 8, core: 2. Of those that a mesh axis runs over, the one named last changes fastest.
Arguments:
- vectors: float32 [32768, 8192], P('prow', 'pcol'), may hold values from -6 to 6
- reflectors: bfloat16 [4, 256, 32768], P(None, 'pcol', 'prow'), may hold values from -0.03125 to 0.03125
- tau_diag: float32 [4, 256], replicated, may hold values from 0.5 to 1.5
- coupling: float32 [4, 256, 256], replicated, may hold values from -0.375 to 0.375
Outputs:
- result: float32 [32768, 8192], P('prow', 'pcol')
All inputs are finite; a program needn't handle non-finite values.
Results may differ from a plain program's by a relative error of at most 0.0003.
Values may be sent and summed in bfloat16 or wider, within the bound.
No kernel may reach another device: no remote copies, remote signals or barrier semaphores. Data moves between devices by JAX's collectives and lax.ppermute only.
A program may use at most 64 MiB of HBM per device.

v0:
```python
import jax
import jax.numpy as jnp
from jax import lax
from jax.sharding import Mesh
from jax.sharding import PartitionSpec as P

PCOL = ("pcol_0", "pcol_1", "pcol_2")


def joined_along(parts, dim):
    lengths = list(parts.shape[1:])
    lengths[dim] *= parts.shape[0]
    return jnp.moveaxis(parts, 0, dim).reshape(lengths)


def stacked_from(x, axes, sequence):
    parts = x[None]
    for k in sequence:
        parts = lax.all_gather(parts, axes[k], axis=0, tiled=True)
    carried = [lax.axis_size(axes[k]) for k in reversed(sequence)]
    parts = parts.reshape(*carried, *x.shape)
    turned = sorted(range(len(sequence)), key=lambda place: sequence[len(sequence) - 1 - place])
    return parts.transpose(*turned, *range(len(sequence), parts.ndim)).reshape(-1, *x.shape)


def gather_axes(x, axes, sequence, dim):
    return joined_along(stacked_from(x, axes, sequence), dim)


def in_blocks(x, dim, devices):
    lengths = x.shape
    parts = x.reshape(*lengths[:dim], devices, lengths[dim] // devices, *lengths[dim + 1 :])
    return jnp.moveaxis(parts, dim, 0)


def sum_at_owner(x, axis, dim):
    parts = in_blocks(x, dim, lax.axis_size(axis))
    arrived = lax.all_to_all(parts, axis, split_axis=0, concat_axis=0, tiled=True)
    return arrived.sum(axis=0)


def copy_for_each(x, axis):
    copies = jnp.broadcast_to(x, (lax.axis_size(axis), *x.shape))
    return lax.all_to_all(copies, axis, split_axis=0, concat_axis=0, tiled=True)


def gather_directly(x, axis, dim):
    return joined_along(copy_for_each(x, axis), dim)


def on_device(vectors, reflectors, tau_diag, coupling):
    count = reflectors.shape[0]
    gathered = gather_axes(reflectors, PCOL, (1, 0, 2), 1)
    current = vectors
    for position in range(count - 1, -1, -1):
        rows_panel = gathered[position]
        widened = rows_panel.astype(jnp.float32)
        tri_factor = jnp.diag(tau_diag[position]) + jnp.triu(coupling[position], 1)
        partial_sum = jnp.dot(
            widened, current, precision=lax.Precision.HIGHEST, preferred_element_type=jnp.float32
        )
        shares = sum_at_owner(partial_sum, "prow", 1)
        local_image = jnp.dot(
            tri_factor, shares, precision=lax.Precision.HIGHEST, preferred_element_type=jnp.float32
        )
        updates = gather_directly(local_image, "prow", 1)
        current = current - lax.dot_general(
            widened,
            updates,
            (((0,), (0,)), ((), ())),
            precision=lax.Precision.HIGHEST,
            preferred_element_type=jnp.float32,
        )
    return current


def solution(mesh):
    finer = Mesh(
        mesh.devices.reshape(mesh.shape["prow"], 8, 4, 2), ("prow", "pcol_0", "pcol_1", "pcol_2")
    )
    placed = (P("prow", PCOL), P(None, PCOL, "prow"), P(), P())
    return jax.shard_map(
        on_device, mesh=finer, in_specs=placed, out_specs=P("prow", PCOL), check_vma=False
    )
```

profile of v0, /device:TPU:2, one launch (start us, length us, event | category | flops | bytes accessed | tf_op | source)
XLA Modules:
  0.0 267.3 jit_solution(2077051281151391013)
XLA Ops:
  6.5 0.0 all-gather.4.cloned.1.call-start
  6.5 18.3 %all-gather = bf16[16,4,4096]{2,1,0:T(4,128)(2,1)} all-gather(bf16[4,4,4096]{2,1,0:T(4,128)(2,1)} %param.5), channel_id=2, replica_groups=mesh['prow'=8,'pcol_0'=8,'pcol_1'=4,'pcol_2'=2] {'pcol_1'}, dimensions={0}, use_global_device_ids=true | all-gather | bytes 655360 | tf_op jit(solution)/shard_map/all_gather | solution.py:19
  24.8 0.0 all-gather.4.cloned.1.call-update
  24.8 0.0 all-gather.6.cloned.1.call-start
  24.9 57.0 %all-gather.4.cloned.1.call-done = bf16[32,4,4,4096]{3,2,1,0:T(4,128)(2,1)} async-done(((bf16[4,4,4,4096]{3,2,1,0:T(4,128)(2,1)}), bf16[32,4,4,4096]{3,2,1,0:T(4,128)(2,1)}) %all-gather.4.cloned.1.call-update) | async-done | bytes 4194320 | tf_op jit(solution)/shard_map/all_gather | solution.py:19
  81.9 0.0 all-gather.6.cloned.1.call-update
  81.9 1.9 copy.20
  83.8 27.2 %all-gather.6.cloned.1.call-done = bf16[64,4,4,4096]{3,2,1,0:T(4,128)(2,1)} async-done(((bf16[32,4,4,4096]{3,2,1,0:T(4,128)(2,1)}), bf16[64,4,4,4096]{3,2,1,0:T(4,128)(2,1)}) %all-gather.6.cloned.1.call-update) | async-done | bytes 8388624 | tf_op jit(solution)/shard_map/all_gather | solution.py:19
  111.0 5.6 %copy.18 = bf16[8,4,2,4,4,4096]{5,4,3,2,1,0:T(4,128)(2,1)S(1)} copy(bf16[8,4,2,4,4,4096]{5,4,3,1,0,2:T(4,128)(2,1)} %bitcast.111) | data formatting | bytes 16777216 | tf_op jit(solution)/shard_map/transpose | solution.py:23
  116.6 5.4 %fusion.36 = (bf16[1,64,4,4096]{3,2,0,1:T(4,128)(2,1)}, bf16[1,64,4,4096]{3,2,0,1:T(4,128)(2,1)}, bf16[1,64,4,4096]{3,2,0,1:T(4,128)(2,1)}, bf16[1,64,4,4096]{3,2,0,1:T(4,128)(2,1)}) fusion(bf16[4,64,4,4096]{3,2,0,1:T(4,128)(2,1)S(1)} %bitcast.109), kind=kLoop, calls=%fused_computation.43 | loop fusion | bytes 16777216 | tf_op jit(solution)/shard_map/slice | solution.py:56
  122.1 4.0 %reshape.56 = bf16[256,4096,1]{1,0,2:T(8,128)(2,1)} reshape(bf16[1,64,4,4096]{3,2,0,1:T(4,128)(2,1)} %get-tuple-element.8) | data formatting | bytes 4194304 | tf_op jit(solution)/shard_map/squeeze | solution.py:56
  126.1 4.6 %convolution_bitcast_fusion.4 = f32[8,256,16]{1,2,0:T(8,128)} fusion(bf16[256,4096,1]{1,0,2:T(8,128)(2,1)} %reshape.56, f32[8,16,4096]{2,1,0:T(8,128)S(1)} %bitcast.110), kind=kOutput, calls=%fused_computation.8 | convolution fusion | flops 1610612736 | bytes 4325376 | tf_op jit(solution)/shard_map/dot_general | solution.py:59
  130.6 7.4 %all-to-all-start = ((f32[8,256,16]{1,2,0:T(8,128)}), f32[8,256,16]{1,2,0:T(8,128)S(1)}, u32[]{:S(2)}, u32[]{:S(2)}) async-start(f32[8,256,16]{1,2,0:T(8,128)} %convolution_bitcast_fusion.4), calls=%async_computation | async-start | bytes 262144 | tf_op jit(solution)/shard_map/all_to_all | solution.py:38
  138.0 9.5 %all-to-all-done = f32[8,256,16]{1,2,0:T(8,128)S(1)} async-done(((f32[8,256,16]{1,2,0:T(8,128)}), f32[8,256,16]{1,2,0:T(8,128)S(1)}, u32[]{:S(2)}, u32[]{:S(2)}) %all-to-all-start) | async-done | bytes 131104 | tf_op jit(solution)/shard_map/all_to_all | solution.py:38
  147.5 0.4 fusion.14
  147.9 0.7 broadcast_in_dim.71
  148.6 3.4 %all-to-all-start.1 = ((f32[8,256,16]{1,2,0:T(8,128)}), f32[8,256,16]{1,2,0:T(8,128)S(1)}, u32[]{:S(2)}, u32[]{:S(2)}) async-start(f32[8,256,16]{1,2,0:T(8,128)} %broadcast_in_dim.71), calls=%async_computation.1 | async-start | bytes 262144 | tf_op jit(solution)/shard_map/all_to_all | solution.py:44
  152.0 4.0 %squeeze.29 = bf16[256,4096]{1,0:T(8,128)(2,1)} reshape(bf16[1,64,4,4096]{3,2,0,1:T(4,128)(2,1)} %get-tuple-element.8) | data formatting | bytes 4194304 | tf_op jit(solution)/shard_map/squeeze | solution.py:56
  156.0 3.9 %squeeze.31 = bf16[256,4096]{1,0:T(8,128)(2,1)} reshape(bf16[1,64,4,4096]{3,2,0,1:T(4,128)(2,1)} %get-tuple-element.7) | data formatting | bytes 4194304 | tf_op jit(solution)/shard_map/squeeze | solution.py:56
  159.9 1.0 all-to-all-done.1
  161.0 2.8 %fusion.3 = f32[4096,128]{0,1:T(8,128)S(1)} fusion(f32[4096,128]{0,1:T(8,128)S(1)} %copy.20, f32[256,128]{0,1:T(8,128)S(1)} %bitcast.113, bf16[256,4096]{1,0:T(8,128)(2,1)} %squeeze.29), kind=kOutput, calls=%fused_computation.7 | convolution fusion | flops 1611137024 | bytes 6422528 | tf_op jit(solution)/shard_map/dot_general | solution.py:67
  163.9 2.2 fusion.38
  166.1 0.0 copy-done
  166.1 15.0 %all_to_all.40 = f32[8,256,16]{1,2,0:T(8,128)S(1)} all-to-all(f32[8,256,16]{1,2,0:T(8,128)S(1)} %bitcast.117), channel_id=1, replica_groups=mesh['prow'=8,'pcol_0'=8,'pcol_1'=4,'pcol_2'=2] {'prow'}, dimensions={0} | all-to-all | bytes 262144 | tf_op jit(solution)/shard_map/all_to_all | solution.py:38
  181.1 0.4 fusion.11
  181.4 0.7 broadcast_in_dim.74
  182.1 3.4 %all-to-all-start.3 = ((f32[8,256,16]{1,2,0:T(8,128)}), f32[8,256,16]{1,2,0:T(8,128)S(1)}, u32[]{:S(2)}, u32[]{:S(2)}) async-start(f32[8,256,16]{1,2,0:T(8,128)} %broadcast_in_dim.74), calls=%async_computation.3 | async-start | bytes 262144 | tf_op jit(solution)/shard_map/all_to_all | solution.py:44
  185.5 2.1 squeeze.33
  187.6 6.9 %all-to-all-done.3 = f32[8,256,16]{1,2,0:T(8,128)S(1)} async-done(((f32[8,256,16]{1,2,0:T(8,128)}), f32[8,256,16]{1,2,0:T(8,128)S(1)}, u32[]{:S(2)}, u32[]{:S(2)}) %all-to-all-start.3) | async-done | bytes 131104 | tf_op jit(solution)/shard_map/all_to_all | solution.py:44
  194.5 3.4 %fusion.2 = f32[4096,128]{0,1:T(8,128)S(1)} fusion(f32[4096,128]{0,1:T(8,128)} %copy-done, f32[256,128]{0,1:T(8,128)S(1)} %bitcast.115, bf16[256,4096]{1,0:T(8,128)(2,1)} %squeeze.31), kind=kOutput, calls=%fused_computation.5 | convolution fusion | flops 1611137024 | bytes 6422528 | tf_op jit(solution)/shard_map/dot_general | solution.py:67
  197.9 2.2 fusion.39
  200.1 11.5 %all_to_all.41 = f32[8,256,16]{1,2,0:T(8,128)S(1)} all-to-all(f32[8,256,16]{1,2,0:T(8,128)S(1)} %bitcast.118), channel_id=1, replica_groups=mesh['prow'=8,'pcol_0'=8,'pcol_1'=4,'pcol_2'=2] {'prow'}, dimensions={0} | all-to-all | bytes 262144 | tf_op jit(solution)/shard_map/all_to_all | solution.py:38
  211.6 0.4 fusion.8
  212.0 0.7 broadcast_in_dim.77
  212.7 3.5 %all-to-all-start.5 = ((f32[8,256,16]{1,2,0:T(8,128)}), f32[8,256,16]{1,2,0:T(8,128)S(1)}, u32[]{:S(2)}, u32[]{:S(2)}) async-start(f32[8,256,16]{1,2,0:T(8,128)} %broadcast_in_dim.77), calls=%async_computation.5 | async-start | bytes 262144 | tf_op jit(solution)/shard_map/all_to_all | solution.py:44
  216.2 4.0 %squeeze.35 = bf16[256,4096]{1,0:T(8,128)(2,1)} reshape(bf16[1,64,4,4096]{3,2,0,1:T(4,128)(2,1)} %get-tuple-element.5) | data formatting | bytes 4194304 | tf_op jit(solution)/shard_map/squeeze | solution.py:56
  220.2 4.9 %all-to-all-done.5 = f32[8,256,16]{1,2,0:T(8,128)S(1)} async-done(((f32[8,256,16]{1,2,0:T(8,128)}), f32[8,256,16]{1,2,0:T(8,128)S(1)}, u32[]{:S(2)}, u32[]{:S(2)}) %all-to-all-start.5) | async-done | bytes 131104 | tf_op jit(solution)/shard_map/all_to_all | solution.py:44
  225.0 2.8 %fusion.1 = f32[4096,128]{0,1:T(8,128)S(1)} fusion(f32[4096,128]{0,1:T(8,128)S(1)} %fusion.2, f32[256,128]{0,1:T(8,128)S(1)} %bitcast.114, bf16[256,4096]{1,0:T(8,128)(2,1)} %squeeze.33), kind=kOutput, calls=%fused_computation.3 | convolution fusion | flops 1611137024 | bytes 6422528 | tf_op jit(solution)/shard_map/dot_general | solution.py:67
  227.9 0.0 copy-start.1
  227.9 0.0 copy-start.5
  227.9 2.2 fusion.40
  230.1 11.6 %all_to_all.42 = f32[8,256,16]{1,2,0:T(8,128)S(1)} all-to-all(f32[8,256,16]{1,2,0:T(8,128)S(1)} %bitcast.119), channel_id=1, replica_groups=mesh['prow'=8,'pcol_0'=8,'pcol_1'=4,'pcol_2'=2] {'prow'}, dimensions={0} | all-to-all | bytes 262144 | tf_op jit(solution)/shard_map/all_to_all | solution.py:38
  241.7 0.4 fusion.5
  242.1 0.1 broadcast_in_dim.80
  242.2 11.5 %all_to_all.43 = f32[8,256,16]{1,2,0:T(8,128)S(1)} all-to-all(f32[8,256,16]{1,2,0:T(8,128)S(1)} %broadcast_in_dim.80), channel_id=1, replica_groups=mesh['prow'=8,'pcol_0'=8,'pcol_1'=4,'pcol_2'=2] {'prow'}, dimensions={0} | all-to-all | bytes 262144 | tf_op jit(solution)/shard_map/all_to_all | solution.py:44
  253.6 0.0 copy-done.5
  253.6 3.9 %fusion = f32[4096,128]{0,1:T(8,128)} fusion(f32[4096,128]{0,1:T(8,128)} %copy-done.1, f32[256,128]{0,1:T(8,128)S(1)} %bitcast.116, bf16[256,4096]{1,0:T(8,128)(2,1)S(1)} %copy-done.5), kind=kOutput, calls=%fused_computation.1 | convolution fusion | flops 1611137024 | bytes 6422528 | tf_op jit(solution)/shard_map/dot_general | solution.py:67
  257.5 2.9 %copy.21 = f32[4096,128]{1,0:T(8,128)} copy(f32[4096,128]{0,1:T(8,128)} %fusion) | data formatting | bytes 4194304 | tf_op jit(solution)/shard_map/sub | solution.py:67
  (19 shorter events, 0.1 us)
Async XLA Ops:
  6.5 75.3 %all-gather.4.cloned.1.call-start = ((), (), s32[]{:S(2)}) async-start(), calls=%async_computation.8 | async-start | bytes 4718592 | tf_op jit(solution)/shard_map/all_gather | solution.py:19
  24.8 86.2 %all-gather.6.cloned.1.call-start = ((), (), s32[]{:S(2)}) async-start(), calls=%async_computation.9 | async-start | bytes 12582912 | tf_op jit(solution)/shard_map/all_gather | solution.py:19
  126.0 11.9 %copy-start.7 = (f32[4,256]{1,0:T(4,128)S(1)}, f32[4,256]{1,0:T(4,128)}, u32[]{:S(2)}) copy-start(f32[4,256]{1,0:T(4,128)} %param.6) | copy-start | bytes 12292
  126.0 21.5 %copy-start.8 = (f32[4,256,256]{2,1,0:T(8,128)S(1)}, f32[4,256,256]{2,1,0:T(8,128)}, u32[]{:S(2)}) copy-start(f32[4,256,256]{2,1,0:T(8,128)} %param.7) | copy-start | bytes 3145732
  130.6 16.9 %all-to-all-start = ((f32[8,256,16]{1,2,0:T(8,128)}), f32[8,256,16]{1,2,0:T(8,128)S(1)}, u32[]{:S(2)}, u32[]{:S(2)}) async-start(f32[8,256,16]{1,2,0:T(8,128)} %convolution_bitcast_fusion.4), calls=%async_computation | async-start | bytes 262144 | tf_op jit(solution)/shard_map/all_to_all | solution.py:38
  148.6 12.4 %all-to-all-start.1 = ((f32[8,256,16]{1,2,0:T(8,128)}), f32[8,256,16]{1,2,0:T(8,128)S(1)}, u32[]{:S(2)}, u32[]{:S(2)}) async-start(f32[8,256,16]{1,2,0:T(8,128)} %broadcast_in_dim.71), calls=%async_computation.1 | async-start | bytes 262144 | tf_op jit(solution)/shard_map/all_to_all | solution.py:44
  161.0 2.9 %copy-start.3 = (bf16[256,4096]{1,0:T(8,128)(2,1)S(1)}, bf16[256,4096]{1,0:T(8,128)(2,1)}, u32[]{:S(2)}) copy-start(bf16[256,4096]{1,0:T(8,128)(2,1)} %squeeze.31) | copy-start | bytes 6291460
  163.8 2.2 copy-start
  163.9 21.7 %copy-start.6 = (bf16[1,64,4,4096]{3,2,0,1:T(4,128)(2,1)S(1)}, bf16[1,64,4,4096]{3,2,0,1:T(4,128)(2,1)}, u32[]{:S(2)}) copy-start(bf16[1,64,4,4096]{3,2,0,1:T(4,128)(2,1)} %get-tuple-element.6) | copy-start | bytes 6291460
  182.1 12.4 %all-to-all-start.3 = ((f32[8,256,16]{1,2,0:T(8,128)}), f32[8,256,16]{1,2,0:T(8,128)S(1)}, u32[]{:S(2)}, u32[]{:S(2)}) async-start(f32[8,256,16]{1,2,0:T(8,128)} %broadcast_in_dim.74), calls=%async_computation.3 | async-start | bytes 262144 | tf_op jit(solution)/shard_map/all_to_all | solution.py:44
  194.5 3.4 %copy-start.2 = (bf16[256,4096]{1,0:T(8,128)(2,1)S(1)}, bf16[256,4096]{1,0:T(8,128)(2,1)}, u32[]{:S(2)}) copy-start(bf16[256,4096]{1,0:T(8,128)(2,1)} %squeeze.33) | copy-start | bytes 6291460
  212.7 12.4 %all-to-all-start.5 = ((f32[8,256,16]{1,2,0:T(8,128)}), f32[8,256,16]{1,2,0:T(8,128)S(1)}, u32[]{:S(2)}, u32[]{:S(2)}) async-start(f32[8,256,16]{1,2,0:T(8,128)} %broadcast_in_dim.77), calls=%async_computation.5 | async-start | bytes 262144 | tf_op jit(solution)/shard_map/all_to_all | solution.py:44
  225.0 2.9 %copy-start.4 = (bf16[256,4096]{1,0:T(8,128)(2,1)S(1)}, bf16[256,4096]{1,0:T(8,128)(2,1)}, u32[]{:S(2)}) copy-start(bf16[256,4096]{1,0:T(8,128)(2,1)} %squeeze.35) | copy-start | bytes 6291460
  227.9 2.3 copy-start.1
  227.9 25.7 %copy-start.5 = (bf16[256,4096]{1,0:T(8,128)(2,1)S(1)}, bf16[256,4096]{1,0:T(8,128)(2,1)}, u32[]{:S(2)}) copy-start(bf16[256,4096]{1,0:T(8,128)(2,1)} %squeeze.35) | copy-start | bytes 6291460
Sparse Core Ops, SparseCore 0:
  24.9 56.8 all-gather.3
  84.0 27.0 all-gather.5
where the time goes:
time: 268 us; the launch traced here: 267 us
  waiting for transfers between devices  107 us (40%)
  blocking collectives  67.7 us (25%)
  local copies, waits for them, and re-layouts  36 us (13%)
  matrix products  25.6 us (10%)
  starting transfers between devices  17.7 us (7%)
  between operations  13.6 us (5%)
    all_gather x2, waiting for transfers between devices, stacked_from(): parts = lax.all_gather(parts, axes[k], axis=0, tiled=True)  84.2 us
    all_to_all x3, blocking collectives, sum_at_owner(): lax.all_to_all(parts, axis, split_axis=0, concat_axis=0, tiled=True)  38 us
    all_gather x1, blocking collectives, stacked_from(): parts = lax.all_gather(parts, axes[k], axis=0, tiled=True)  18.3 us
    squeeze x5, local copies, waits for them, and re-layouts, on_device(): rows_panel = gathered[position]  17.9 us
    dot_general x4, matrix products, on_device(): lax.dot_general(widened, updates, (((0,), (0,)), ((), ())), precision=lax...  12.9 us
    all_to_all x3, waiting for transfers between devices, copy_for_each(): return lax.all_to_all(copies, axis, split_axis=0, concat_axis=0, tiled=True)  12.8 us
    all_to_all x1, blocking collectives, copy_for_each(): return lax.all_to_all(copies, axis, split_axis=0, concat_axis=0, tiled=True)  11.5 us
    dot_general x4, matrix products, on_device(): jnp.dot(widened, current, precision=lax.Precision.HIGHEST, preferred_elem...  11.2 us
  transfers between devices with their start and end apart: 6, of which 6 were waited for; matrix products, arithmetic and copies ran while one was open for 6% of the time, Pallas kernels for 0%

commit v1 on v0

--- a/solution.py
+++ b/solution.py
@@ -16,7 +16,16 @@
 def stacked_from(x, axes, sequence):
     parts = x[None]
     for k in sequence:
-        parts = lax.all_gather(parts, axes[k], axis=0, tiled=True)
+        z_in = axes[k]
+        parts = jnp.concatenate(
+            jax.lax.all_to_all(
+                jnp.stack([parts] * jax.lax.axis_size(z_in), axis=0),
+                axis_name=z_in,
+                concat_axis=0,
+                split_axis=0,
+            ),
+            0,
+        )
     carried = [lax.axis_size(axes[k]) for k in reversed(sequence)]
     parts = parts.reshape(*carried, *x.shape)
     turned = sorted(range(len(sequence)), key=lambda place: sequence[len(sequence) - 1 - place])

time: 268 us -> 298 us (1.11)
  local copies, waits for them, and re-layouts: 36 us -> 52.8 us
  between operations: 13.6 us -> 0.24 us
  starting transfers between devices: 17.7 us -> 28.8 us
  other arithmetic: 0.05 us -> 7.94 us
  waiting for transfers between devices: 107 us -> 112 us
    all_to_all x0 -> x1, waiting for transfers between devices: none -> 93.4 us  [stacked_from(): jax.lax.all_to_all(jnp.stack([parts] * jax.lax.axis_size(z_in), axis=0),...]
    all_gather x2 -> x0, waiting for transfers between devices: 84.2 us -> none  [stacked_from(): parts = lax.all_gather(parts, axes[k], axis=0, tiled=True)]
    all_gather x1 -> x0, blocking collectives: 18.3 us -> none  [stacked_from(): parts = lax.all_gather(parts, axes[k], axis=0, tiled=True)]
    all_to_all x1 -> x2, blocking collectives: 11.5 us -> 25.4 us  [stacked_from(): jax.lax.all_to_all(jnp.stack([parts] * jax.lax.axis_size(z_in), axis=0),...]
    squeeze x5 -> x8, local copies, waits for them, and re-layouts: 17.9 us -> 30.3 us  [on_device(): rows_panel = gathered[position]]
    another operation x0 -> x3, local copies, waits for them, and re-layouts: none -> 9.42 us  [the longest x2 5.17 us: stacked_from(): jnp.stack([parts] * jax.lax.axis_size(z_in), axis=0)]
    another operation x0 -> x1, other arithmetic: none -> 7.89 us  [stacked_from(): jnp.stack([parts] * jax.lax.axis_size(z_in), axis=0)]
    transpose x1 -> x0, local copies, waits for them, and re-layouts: 5.62 us -> none  [stacked_from(): parts.transpose(*turned, *range(len(sequence), parts.ndim))]
  transfers between devices with their start and end apart: 6 -> 6, of which waited for: 6 -> 6; matrix products, arithmetic and copies ran while one was open for 6% -> 10% of each run, Pallas kernels for 0% -> 0%
where the time goes in v1:
time: 298 us; the launch traced here: 296 us
  waiting for transfers between devices  112 us (38%)
  blocking collectives  68.5 us (23%)
  local copies, waits for them, and re-layouts  52.8 us (18%)
  starting transfers between devices  28.8 us (10%)
  matrix products  25.6 us (9%)
  other arithmetic  7.94 us (3%)
    all_to_all x1, waiting for transfers between devices, stacked_from(): jax.lax.all_to_all(jnp.stack([parts] * jax.lax.axis_size(z_in), axis=0),...  93.4 us
    all_to_all x3, blocking collectives, sum_at_owner(): lax.all_to_all(parts, axis, split_axis=0, concat_axis=0, tiled=True)  43.2 us
    squeeze x8, local copies, waits for them, and re-layouts, on_device(): rows_panel = gathered[position]  30.3 us
    all_to_all x2, blocking collectives, stacked_from(): jax.lax.all_to_all(jnp.stack([parts] * jax.lax.axis_size(z_in), axis=0),...  25.4 us
    all_to_all x4, starting transfers between devices, copy_for_each(): return lax.all_to_all(copies, axis, split_axis=0, concat_axis=0, tiled=True)  13.7 us
    dot_general x4, matrix products, on_device(): lax.dot_general(widened, updates, (((0,), (0,)), ((), ())), precision=lax...  13 us
    dot_general x4, matrix products, on_device(): jnp.dot(widened, current, precision=lax.Precision.HIGHEST, preferred_elem...  11.2 us
    all_to_all x1, starting transfers between devices, sum_at_owner(): lax.all_to_all(parts, axis, split_axis=0, concat_axis=0, tiled=True)  10.3 us
  transfers between devices with their start and end apart: 6, of which 6 were waited for; matrix products, arithmetic and copies ran while one was open for 10% of the time, Pallas kernels for 0%

profile of v1, /device:TPU:2, one launch (start us, length us, event | category | flops | bytes accessed | tf_op | source)
XLA Modules:
  0.0 296.2 jit_solution(2634276168764888323)
XLA Ops:
  0.0 1.1 stack.9
  1.1 14.9 %all_to_all.55 = bf16[4,1,4,4,4096]{4,3,2,1,0:T(4,128)(2,1)S(1)} all-to-all(bf16[4,1,4,4,4096]{4,3,2,1,0:T(4,128)(2,1)S(1)} %stack.9), channel_id=1, replica_groups=mesh['prow'=8,'pcol_0'=8,'pcol_1'=4,'pcol_2'=2] {'pcol_1'}, dimensions={0} | all-to-all | bytes 1048576 | tf_op jit(solution)/shard_map/all_to_all | solution.py:21
  16.0 4.1 %stack.10 = bf16[8,4,4,4,4096]{4,3,2,1,0:T(4,128)(2,1)} broadcast(bf16[4,4,4,4096]{3,2,1,0:T(4,128)(2,1)S(1)} %bitcast.106), dimensions={1,2,3,4} | broadcast | bytes 4718592 | tf_op jit(solution)/shard_map/stack | solution.py:22
  20.1 4.8 %all-to-all-start.1 = ((bf16[8,4,4,4,4096]{4,3,2,1,0:T(4,128)(2,1)}), bf16[8,4,4,4,4096]{4,3,2,1,0:T(4,128)(2,1)}, u32[]{:S(2)}, u32[]{:S(2)}) async-start(bf16[8,4,4,4,4096]{4,3,2,1,0:T(4,128)(2,1)} %stack.10), calls=%async_computation.1 | async-start | bytes 8388608 | tf_op jit(solution)/shard_map/all_to_all | solution.py:21
  24.9 1.9 copy.23
  26.9 93.4 %all-to-all-done.1 = bf16[8,4,4,4,4096]{4,3,2,1,0:T(4,128)(2,1)} async-done(((bf16[8,4,4,4,4096]{4,3,2,1,0:T(4,128)(2,1)}), bf16[8,4,4,4,4096]{4,3,2,1,0:T(4,128)(2,1)}, u32[]{:S(2)}, u32[]{:S(2)}) %all-to-all-start.1) | async-done | bytes 4194336 | tf_op jit(solution)/shard_map/all_to_all | solution.py:21
  120.2 7.9 %pad_maximum_fusion = bf16[2,32,4,4,4096]{4,3,2,1,0:T(4,128)(2,1)S(1)} fusion(bf16[1,32,4,4,4096]{4,3,2,1,0:T(4,128)(2,1)} %bitcast.1), kind=kLoop, calls=%fused_computation | loop fusion | flops 4194304 | bytes 12582912 | tf_op jit(solution)/shard_map/stack | solution.py:22
  128.1 10.5 %all_to_all.56 = bf16[2,32,4,4,4096]{4,3,2,1,0:T(4,128)(2,1)S(1)} all-to-all(bf16[2,32,4,4,4096]{4,3,2,1,0:T(4,128)(2,1)S(1)} %pad_maximum_fusion), channel_id=1, replica_groups=mesh['prow'=8,'pcol_0'=8,'pcol_1'=4,'pcol_2'=2] {'pcol_2'}, dimensions={0} | all-to-all | bytes 16777216 | tf_op jit(solution)/shard_map/all_to_all | solution.py:21
  138.6 4.2 %copy.21 = bf16[2,8,4,4,4,4096]{5,4,3,0,2,1:T(4,128)(2,1)S(1)} copy(bf16[2,8,4,4,4,4096]{5,4,3,2,1,0:T(4,128)(2,1)S(1)} %bitcast.101) | data formatting | bytes 16777216 | tf_op jit(solution)/shard_map/reshape;reshape | solution.py:30
  142.9 5.4 %fusion.32 = (bf16[1,64,4,4096]{3,2,0,1:T(4,128)(2,1)}, bf16[1,64,4,4096]{3,2,0,1:T(4,128)(2,1)}, bf16[1,64,4,4096]{3,2,0,1:T(4,128)(2,1)}, bf16[1,64,4,4096]{3,2,0,1:T(4,128)(2,1)}) fusion(bf16[4,64,4,4096]{3,2,0,1:T(4,128)(2,1)S(1)} %bitcast.100), kind=kLoop, calls=%fused_computation.43 | loop fusion | bytes 16777216 | tf_op jit(solution)/shard_map/slice | solution.py:65
  148.3 4.0 %reshape.49 = bf16[256,4096,1]{1,0,2:T(8,128)(2,1)} reshape(bf16[1,64,4,4096]{3,2,0,1:T(4,128)(2,1)} %get-tuple-element.8) | data formatting | bytes 4194304 | tf_op jit(solution)/shard_map/squeeze | solution.py:65
  152.3 4.6 %convolution_bitcast_fusion.3 = f32[8,256,16]{1,2,0:T(8,128)} fusion(bf16[256,4096,1]{1,0,2:T(8,128)(2,1)} %reshape.49, f32[8,16,4096]{2,1,0:T(8,128)S(1)} %bitcast.105), kind=kOutput, calls=%fused_computation.8 | convolution fusion | flops 1610612736 | bytes 4325376 | tf_op jit(solution)/shard_map/dot_general | solution.py:68
  156.8 10.3 %all-to-all-start.3 = ((f32[8,256,16]{1,2,0:T(8,128)}), f32[8,256,16]{1,2,0:T(8,128)S(1)}, u32[]{:S(2)}, u32[]{:S(2)}) async-start(f32[8,256,16]{1,2,0:T(8,128)} %convolution_bitcast_fusion.3), calls=%async_computation.3 | async-start | bytes 262144 | tf_op jit(solution)/shard_map/all_to_all | solution.py:47
  167.2 9.4 %all-to-all-done.3 = f32[8,256,16]{1,2,0:T(8,128)S(1)} async-done(((f32[8,256,16]{1,2,0:T(8,128)}), f32[8,256,16]{1,2,0:T(8,128)S(1)}, u32[]{:S(2)}, u32[]{:S(2)}) %all-to-all-start.3) | async-done | bytes 131104 | tf_op jit(solution)/shard_map/all_to_all | solution.py:47
  176.6 0.4 fusion.10
  176.9 0.7 broadcast_in_dim.67
  177.6 3.4 %all-to-all-start.4 = ((f32[8,256,16]{1,2,0:T(8,128)}), f32[8,256,16]{1,2,0:T(8,128)S(1)}, u32[]{:S(2)}, u32[]{:S(2)}) async-start(f32[8,256,16]{1,2,0:T(8,128)} %broadcast_in_dim.67), calls=%async_computation.4 | async-start | bytes 262144 | tf_op jit(solution)/shard_map/all_to_all | solution.py:53
  181.0 4.0 %squeeze.28 = bf16[256,4096]{1,0:T(8,128)(2,1)} reshape(bf16[1,64,4,4096]{3,2,0,1:T(4,128)(2,1)} %get-tuple-element.8) | data formatting | bytes 4194304 | tf_op jit(solution)/shard_map/squeeze | solution.py:65
  185.0 4.0 %reshape.50 = bf16[256,4096,1]{1,0,2:T(8,128)(2,1)} reshape(bf16[1,64,4,4096]{3,2,0,1:T(4,128)(2,1)} %get-tuple-element.7) | data formatting | bytes 4194304 | tf_op jit(solution)/shard_map/squeeze | solution.py:65
  189.0 1.0 all-to-all-done.4
  190.0 2.8 convolution_subtract_fusion.3
  192.9 2.2 convolution_bitcast_fusion.2
  195.1 15.0 %all_to_all.57 = f32[8,256,16]{1,2,0:T(8,128)S(1)} all-to-all(f32[8,256,16]{1,2,0:T(8,128)S(1)} %convolution_bitcast_fusion.2), channel_id=1, replica_groups=mesh['prow'=8,'pcol_0'=8,'pcol_1'=4,'pcol_2'=2] {'prow'}, dimensions={0} | all-to-all | bytes 262144 | tf_op jit(solution)/shard_map/all_to_all | solution.py:47
  210.1 0.4 fusion.7
  210.5 0.7 broadcast_in_dim.70
  211.2 3.5 %all-to-all-start.6 = ((f32[8,256,16]{1,2,0:T(8,128)}), f32[8,256,16]{1,2,0:T(8,128)S(1)}, u32[]{:S(2)}, u32[]{:S(2)}) async-start(f32[8,256,16]{1,2,0:T(8,128)} %broadcast_in_dim.70), calls=%async_computation.6 | async-start | bytes 262144 | tf_op jit(solution)/shard_map/all_to_all | solution.py:53
  214.8 4.2 %squeeze.30 = bf16[256,4096]{1,0:T(8,128)(2,1)} reshape(bf16[1,64,4,4096]{3,2,0,1:T(4,128)(2,1)} %get-tuple-element.7) | data formatting | bytes 4194304 | tf_op jit(solution)/shard_map/squeeze | solution.py:65
  219.0 2.0 reshape.51
  221.0 2.6 all-to-all-done.6
  223.6 3.4 %convolution_subtract_fusion.2 = f32[4096,128]{0,1:T(8,128)S(1)} fusion(f32[4096,128]{0,1:T(8,128)} %copy-done.2, bf16[256,4096]{1,0:T(8,128)(2,1)} %squeeze.30, f32[256,128]{0,1:T(8,128)S(1)} %bitcast.109), kind=kOutput, calls=%fused_computation.3 | convolution fusion | flops 1611137024 | bytes 6422528 | tf_op jit(solution)/shard_map/dot_general | solution.py:76
  227.0 2.2 convolution_bitcast_fusion.1
  229.2 13.2 %all_to_all.58 = f32[8,256,16]{1,2,0:T(8,128)S(1)} all-to-all(f32[8,256,16]{1,2,0:T(8,128)S(1)} %convolution_bitcast_fusion.1), channel_id=1, replica_groups=mesh['prow'=8,'pcol_0'=8,'pcol_1'=4,'pcol_2'=2] {'prow'}, dimensions={0} | all-to-all | bytes 262144 | tf_op jit(solution)/shard_map/all_to_all | solution.py:47
  242.5 0.4 fusion.4
  242.8 0.7 broadcast_in_dim.73
  243.5 3.4 %all-to-all-start.8 = ((f32[8,256,16]{1,2,0:T(8,128)}), f32[8,256,16]{1,2,0:T(8,128)S(1)}, u32[]{:S(2)}, u32[]{:S(2)}) async-start(f32[8,256,16]{1,2,0:T(8,128)} %broadcast_in_dim.73), calls=%async_computation.8 | async-start | bytes 262144 | tf_op jit(solution)/shard_map/all_to_all | solution.py:53
  246.9 4.0 %squeeze.32 = bf16[256,4096]{1,0:T(8,128)(2,1)} reshape(bf16[1,64,4,4096]{3,2,0,1:T(4,128)(2,1)} %get-tuple-element.6) | data formatting | bytes 4194304 | tf_op jit(solution)/shard_map/squeeze | solution.py:65
  250.9 3.9 %reshape.52 = bf16[256,4096,1]{1,0,2:T(8,128)(2,1)} reshape(bf16[1,64,4,4096]{3,2,0,1:T(4,128)(2,1)} %get-tuple-element.5) | data formatting | bytes 4194304 | tf_op jit(solution)/shard_map/squeeze | solution.py:65
  254.8 1.1 all-to-all-done.8
  255.9 2.8 convolution_subtract_fusion.1
  258.8 2.2 convolution_bitcast_fusion
  261.0 14.9 %all_to_all.59 = f32[8,256,16]{1,2,0:T(8,128)S(1)} all-to-all(f32[8,256,16]{1,2,0:T(8,128)S(1)} %convolution_bitcast_fusion), channel_id=1, replica_groups=mesh['prow'=8,'pcol_0'=8,'pcol_1'=4,'pcol_2'=2] {'prow'}, dimensions={0} | all-to-all | bytes 262144 | tf_op jit(solution)/shard_map/all_to_all | solution.py:47
  275.9 0.4 fusion.1
  276.3 0.7 broadcast_in_dim.76
  277.0 3.4 %all-to-all-start.10 = ((f32[8,256,16]{1,2,0:T(8,128)}), f32[8,256,16]{1,2,0:T(8,128)S(1)}, u32[]{:S(2)}, u32[]{:S(2)}) async-start(f32[8,256,16]{1,2,0:T(8,128)} %broadcast_in_dim.76), calls=%async_computation.10 | async-start | bytes 262144 | tf_op jit(solution)/shard_map/all_to_all | solution.py:53
  280.4 4.1 %squeeze.34 = bf16[256,4096]{1,0:T(8,128)(2,1)} reshape(bf16[1,64,4,4096]{3,2,0,1:T(4,128)(2,1)} %get-tuple-element.5) | data formatting | bytes 4194304 | tf_op jit(solution)/shard_map/squeeze | solution.py:65
  284.5 4.9 %all-to-all-done.10 = f32[8,256,16]{1,2,0:T(8,128)S(1)} async-done(((f32[8,256,16]{1,2,0:T(8,128)}), f32[8,256,16]{1,2,0:T(8,128)S(1)}, u32[]{:S(2)}, u32[]{:S(2)}) %all-to-all-start.10) | async-done | bytes 131104 | tf_op jit(solution)/shard_map/all_to_all | solution.py:53
  289.4 3.9 %convolution_subtract_fusion = f32[4096,128]{0,1:T(8,128)} fusion(f32[4096,128]{0,1:T(8,128)S(1)} %copy-done.1, bf16[256,4096]{1,0:T(8,128)(2,1)} %squeeze.34, f32[256,128]{0,1:T(8,128)S(1)} %bitcast.110), kind=kOutput, calls=%fused_computation.1 | convolution fusion | flops 1611137024 | bytes 6422528 | tf_op jit(solution)/shard_map/dot_general | solution.py:76
  293.3 2.9 copy.25
  (23 shorter events, 0.1 us)
Async XLA Ops:
  20.1 100.1 %all-to-all-start.1 = ((bf16[8,4,4,4,4096]{4,3,2,1,0:T(4,128)(2,1)}), bf16[8,4,4,4,4096]{4,3,2,1,0:T(4,128)(2,1)}, u32[]{:S(2)}, u32[]{:S(2)}) async-start(bf16[8,4,4,4,4096]{4,3,2,1,0:T(4,128)(2,1)} %stack.10), calls=%async_computation.1 | async-start | bytes 8388608 | tf_op jit(solution)/shard_map/all_to_all | solution.py:21
  152.3 14.9 %copy-start.7 = (f32[4,256]{1,0:T(4,128)S(1)}, f32[4,256]{1,0:T(4,128)}, u32[]{:S(2)}) copy-start(f32[4,256]{1,0:T(4,128)} %param.6) | copy-start | bytes 12292
  152.3 24.3 %copy-start.8 = (f32[4,256,256]{2,1,0:T(8,128)S(1)}, f32[4,256,256]{2,1,0:T(8,128)}, u32[]{:S(2)}) copy-start(f32[4,256,256]{2,1,0:T(8,128)} %param.7) | copy-start | bytes 3145732
  156.8 19.7 %all-to-all-start.3 = ((f32[8,256,16]{1,2,0:T(8,128)}), f32[8,256,16]{1,2,0:T(8,128)S(1)}, u32[]{:S(2)}, u32[]{:S(2)}) async-start(f32[8,256,16]{1,2,0:T(8,128)} %convolution_bitcast_fusion.3), calls=%async_computation.3 | async-start | bytes 262144 | tf_op jit(solution)/shard_map/all_to_all | solution.py:47
  177.6 12.4 %all-to-all-start.4 = ((f32[8,256,16]{1,2,0:T(8,128)}), f32[8,256,16]{1,2,0:T(8,128)S(1)}, u32[]{:S(2)}, u32[]{:S(2)}) async-start(f32[8,256,16]{1,2,0:T(8,128)} %broadcast_in_dim.67), calls=%async_computation.4 | async-start | bytes 262144 | tf_op jit(solution)/shard_map/all_to_all | solution.py:53
  190.0 2.9 copy-start.4
  192.9 2.3 copy-start.2
  211.2 12.4 %all-to-all-start.6 = ((f32[8,256,16]{1,2,0:T(8,128)}), f32[8,256,16]{1,2,0:T(8,128)S(1)}, u32[]{:S(2)}, u32[]{:S(2)}) async-start(f32[8,256,16]{1,2,0:T(8,128)} %broadcast_in_dim.70), calls=%async_computation.6 | async-start | bytes 262144 | tf_op jit(solution)/shard_map/all_to_all | solution.py:53
  214.8 4.2 %copy-start.3 = (bf16[1,64,4,4096]{3,2,0,1:T(4,128)(2,1)S(1)}, bf16[1,64,4,4096]{3,2,0,1:T(4,128)(2,1)}, u32[]{:S(2)}) copy-start(bf16[1,64,4,4096]{3,2,0,1:T(4,128)(2,1)} %get-tuple-element.6) | copy-start | bytes 6291460
  223.6 3.4 %copy-start.5 = (bf16[256,4096,1]{1,0,2:T(8,128)(2,1)S(1)}, bf16[256,4096,1]{1,0,2:T(8,128)(2,1)}, u32[]{:S(2)}) copy-start(bf16[256,4096,1]{1,0,2:T(8,128)(2,1)} %reshape.51) | copy-start | bytes 6291460
  243.5 12.4 %all-to-all-start.8 = ((f32[8,256,16]{1,2,0:T(8,128)}), f32[8,256,16]{1,2,0:T(8,128)S(1)}, u32[]{:S(2)}, u32[]{:S(2)}) async-start(f32[8,256,16]{1,2,0:T(8,128)} %broadcast_in_dim.73), calls=%async_computation.8 | async-start | bytes 262144 | tf_op jit(solution)/shard_map/all_to_all | solution.py:53
  255.9 2.9 copy-start.6
  258.8 2.3 copy-start
  277.0 12.4 %all-to-all-start.10 = ((f32[8,256,16]{1,2,0:T(8,128)}), f32[8,256,16]{1,2,0:T(8,128)S(1)}, u32[]{:S(2)}, u32[]{:S(2)}) async-start(f32[8,256,16]{1,2,0:T(8,128)} %broadcast_in_dim.76), calls=%async_computation.10 | async-start | bytes 262144 | tf_op jit(solution)/shard_map/all_to_all | solution.py:53
  280.4 9.0 %copy-start.1 = (f32[4096,128]{0,1:T(8,128)S(1)}, f32[4096,128]{0,1:T(8,128)}, u32[]{:S(2)}) copy-start(f32[4096,128]{0,1:T(8,128)} %copy-done) | copy-start | bytes 6291460
